TPU v7x, 32 devices: a whole 2x2x4 slice. The times are simulated.
32 devices in a mesh: sp: 8 (over z, x), tp: 4 (over y, core).
Axes of the slice: x: 2, y: 2, z: 4, core: 2. Of those that a mesh axis runs over, the one named last changes fastest.
Arguments:
- prefill_keys: bfloat16 [2, 8, 512, 8, 128], P(None, None, 'sp', 'tp'), may hold values from -6 to 6
- prefill_values: bfloat16 [2, 8, 512, 8, 128], P(None, None, 'sp', 'tp'), may hold values from -6 to 6
- prompt_lengths: int32 [8], replicated, may hold values from 1 to 512, 2048 in all
- destination: int32 [8], replicated, may hold values from 0 to 7, each once
- page_table: int32 [8, 32], P('sp'), may hold values from 0 to 31, as said below
- queries: bfloat16 [2, 8, 64, 128], P(None, 'sp', 'tp'), may hold values from -6 to 6
Outputs:
- key_pages: bfloat16 [2, 256, 16, 8, 128], P(None, 'sp', None, 'tp')
- value_pages: bfloat16 [2, 256, 16, 8, 128], P(None, 'sp', None, 'tp')
- attended: bfloat16 [2, 8, 64, 128], P(None, 'sp')
Inputs may be any that keep to these rules, and one draw needn't show every extreme that they name: `destination`: each slot is named by exactly one prompt; slot s is held by sp index s // 1. `page_table`: the rows of the 1 slots of one sp index together name each of that index's 1 times 32 local pool pages exactly once.
All inputs are finite; a program needn't handle non-finite values.
Results may differ from a plain program's by a relative error of at most 0.0085.
Values may be sent and summed in bfloat16 or wider, within the bound.
A program may use at most 128 MiB of HBM per device.

v0:
```python
import functools

import jax
import jax.numpy as jnp
from jax import lax
from jax.experimental import pallas as pl
from jax.experimental.pallas import tpu as pltpu
from jax.sharding import PartitionSpec as P

MESH = pl.DeviceIdType.MESH


def partner(me, step, n, way=1):
    if n & (n - 1):
        return lax.rem(me + way * step + n, n)
    total, bit = 0, 1
    while bit < n:
        total = total + ((me // bit + step // bit) % 2) * bit
        bit *= 2
    return total


def turn(me, step, n):
    if n & (n - 1) or n < 4:
        return step
    outer = (me // (n // 4) + me // (n // 2) + 1) % 2
    crossing = step // (n // 2)
    return step + crossing * ((step + outer * (n // 4)) % (n // 2) + n // 2 - step)


def kernel(
    sp_size, tp_size, page_size,
    lengths, destination, table, queries, keys_in, values_in,
    key_pages, value_pages, attended,
    fetched, outbox, inboxes, heads_out, inverse,
    fetch_sem, send_sem, recv_sem, head_send_sem, head_recv_sem,
):
    layers, prompts, rows, head_size = keys_in.shape
    per_block, page_rows = outbox.shape[3], outbox.shape[4]
    heads_here = page_rows // page_size
    pages = table.shape[1]
    query_heads = queries.shape[1]
    me, row = lax.axis_index("sp"), lax.axis_index("tp")

    def head_copy(layer, step):
        other = lax.rem(row + step, tp_size)
        return pltpu.make_async_remote_copy(
            src_ref=heads_out.at[layer, row],
            dst_ref=heads_out.at[layer, row],
            send_sem=head_send_sem.at[layer, step],
            recv_sem=head_recv_sem.at[layer, step],
            device_id={"tp": other},
            device_id_type=MESH,
        )

    def block_copy(layer, step):
        other = partner(me, step, sp_size)
        return pltpu.make_async_remote_copy(
            src_ref=outbox.at[layer, other],
            dst_ref=inboxes[layer].at[me],
            send_sem=send_sem.at[layer, step],
            recv_sem=recv_sem.at[layer, step],
            device_id={"sp": other},
            device_id_type=MESH,
        )

    fetches = []
    for layer in range(layers):
        for kind, source in enumerate((keys_in, values_in)):
            fetch = pltpu.make_async_copy(
                source.at[layer], fetched.at[layer, kind], fetch_sem.at[layer, kind]
            )
            fetch.start()
            fetches.append(fetch)

    barrier = pltpu.get_barrier_semaphore()

    def greet_sp(step, carry):
        pl.semaphore_signal(
            barrier, inc=1, device_id={"sp": partner(me, step, sp_size)}, device_id_type=MESH
        )
        return carry

    lax.fori_loop(1, sp_size, greet_sp, 0)
    for step in range(1, tp_size):
        pl.semaphore_signal(
            barrier, inc=1, device_id={"tp": lax.rem(row + step, tp_size)}, device_id_type=MESH
        )

    def holder_of(slot):
        def look(prompt, found):
            return jnp.where(destination[prompt] == slot, prompt, found)

        return lax.fori_loop(0, prompts, look, jnp.int32(0), unroll=prompts <= 8)

    my_len = lengths[holder_of(me)]
    for fetch in fetches:
        fetch.wait()

    def fill(step, carry):
        other = partner(me, step, sp_size)
        held = holder_of(other)
        for layer in range(layers):
            for kind in range(2):
                block = fetched[layer, kind, held]
                outbox[layer, other, kind] = block.reshape(per_block, page_rows, head_size)
        return carry

    lax.fori_loop(1, sp_size, fill, 0)
    own = holder_of(me)
    for layer in range(layers):
        for kind in range(2):
            block = fetched[layer, kind, own]
            inboxes[layer][me, kind] = block.reshape(per_block, page_rows, head_size)

    pl.semaphore_wait(barrier, sp_size - 1 + tp_size - 1)

    for layer in range(layers):
        def send(step, carry):
            block_copy(layer, turn(me, step, sp_size)).start()
            return carry

        lax.fori_loop(1, sp_size, send, 0)

    def invert(page, carry):
        def look(position, found):
            return jnp.where(table[0, position] == page, position, found)

        inverse[page] = lax.fori_loop(0, pages, look, jnp.int32(0), unroll=pages <= 32)
        return carry

    lax.fori_loop(0, pages, invert, 0)

    groups = query_heads // heads_here
    shape = (query_heads, rows)
    column = lax.broadcasted_iota(jnp.int32, shape, 1)
    column_head, column_token = column % heads_here, column // heads_here
    same_head = lax.broadcasted_iota(jnp.int32, shape, 0) // groups == column_head
    page_token = lax.broadcasted_iota(jnp.int32, (page_rows, head_size), 0) // heads_here
    scale = head_size ** (-0.5)
    tokens = rows // heads_here

    for layer in range(layers):
        asked = queries[layer]

        def attend(step, carry):
            top, total, mixed = carry
            step = turn(me, step, sp_size)
            source = partner(me, step, sp_size, -1)

            @pl.when(step > 0)
            def _():
                block_copy(layer, step).wait_recv()

            block_keys = inboxes[layer][source, 0].reshape(rows, head_size)
            block_values = inboxes[layer][source, 1].reshape(rows, head_size)
            scores = lax.dot_general(
                asked, block_keys, (((1,), (1,)), ((), ())), preferred_element_type=jnp.float32
            ) * scale
            seen = same_head & (column_token + source * tokens < my_len)
            scores = jnp.where(seen, scores, -1e30)
            new_top = jnp.maximum(top, jnp.max(scores, axis=1, keepdims=True))
            fade = jnp.exp(top - new_top)
            weights = jnp.exp(scores - new_top)
            high = weights.astype(jnp.bfloat16)
            low = (weights - high.astype(jnp.float32)).astype(jnp.bfloat16)
            part = jnp.dot(high, block_values, preferred_element_type=jnp.float32) + jnp.dot(
                low, block_values, preferred_element_type=jnp.float32
            )
            total = total * fade + jnp.sum(weights, axis=1, keepdims=True)
            return new_top, total, mixed * fade + part

        _, total, mixed = lax.fori_loop(
            0, sp_size, attend,
            (
                jnp.full((query_heads, 1), -1e30, jnp.float32),
                jnp.zeros((query_heads, 1), jnp.float32),
                jnp.zeros((query_heads, head_size), jnp.float32),
            ),
        )
        heads_out[layer, row] = (mixed / total).astype(jnp.bfloat16)

        def place(page, carry):
            position = inverse[page]
            source, within = position // per_block, position % per_block
            inside = page_token + position * page_size < my_len
            for kind, target in enumerate((key_pages, value_pages)):
                content = inboxes[layer][source, kind, within]
                target[layer, page] = jnp.where(inside, content, jnp.zeros_like(content))
            return carry

        early = pages // 8
        lax.fori_loop(0, early, place, 0, unroll=early <= 4)
        for step in range(1, tp_size):
            head_copy(layer, step).start()
        lax.fori_loop(early, pages, place, 0, unroll=4)

    for layer in range(layers):
        def sent(step, carry):
            block_copy(layer, step).wait_send()
            return carry

        lax.fori_loop(1, sp_size, sent, 0)
    for layer in range(layers):
        for step in range(1, tp_size):
            head_copy(layer, step).wait()
        attended[layer] = heads_out[layer].reshape(tp_size * query_heads, head_size)


def write_out(*refs):
    sources, targets, sems = refs[:3], refs[3:6], refs[6]
    copies = [
        pltpu.make_async_copy(sources[i], targets[i], sems.at[i]) for i in range(3)
    ]
    for copy in copies:
        copy.start()
    for copy in copies:
        copy.wait()


def local(sp_size, tp_size, prefill_keys, prefill_values, prompt_lengths, destination, page_table, queries):
    layers, prompts, tokens, heads_here, head_size = prefill_keys.shape
    slots_here, pages = page_table.shape
    query_heads = queries.shape[2]
    page_size = tokens * sp_size // pages
    rows, page_rows = tokens * heads_here, page_size * heads_here
    per_block = tokens // page_size
    assert slots_here == 1 and per_block * page_size == tokens
    flat = (layers, prompts, rows, head_size)
    paged = (layers, pages, page_rows, head_size)
    shapes = (paged, paged, (layers, tp_size * query_heads, head_size))
    everywhere = pl.BlockSpec(memory_space=pl.ANY)
    scalars = pl.BlockSpec(memory_space=pltpu.SMEM)
    vectors = pl.BlockSpec(memory_space=pltpu.VMEM)
    boxes = (layers, sp_size, 2, per_block, page_rows, head_size)
    kind = prefill_keys.dtype
    dma = pltpu.SemaphoreType.DMA
    grant = min(60 * 1024 * 1024, 67043328 - 2 * prefill_keys.size * kind.itemsize - (1 << 20))
    results = pl.pallas_call(
        functools.partial(kernel, sp_size, tp_size, page_size),
        out_shape=tuple(pltpu.VMEM(shape, kind) for shape in shapes),
        in_specs=[scalars, scalars, scalars, vectors, everywhere, everywhere],
        out_specs=(vectors, vectors, vectors),
        scratch_shapes=[
            pltpu.VMEM((layers, 2, prompts, rows, head_size), kind),
            pltpu.VMEM(boxes, kind),
            (pltpu.VMEM(boxes[1:], kind),) * layers,
            pltpu.VMEM((layers, tp_size, query_heads, head_size), jnp.bfloat16),
            pltpu.SMEM((pages,), jnp.int32),
            dma((layers, 2)),
            dma((layers, sp_size)),
            dma((layers, sp_size)),
            dma((layers, tp_size)),
            dma((layers, tp_size)),
        ],
        compiler_params=pltpu.CompilerParams(
            collective_id=0, has_side_effects=True, vmem_limit_bytes=grant
        ),
    )(
        prompt_lengths,
        destination,
        page_table,
        queries.reshape(layers, query_heads, head_size),
        prefill_keys.reshape(flat),
        prefill_values.reshape(flat),
    )
    key_pages, value_pages, attended = pl.pallas_call(
        write_out,
        out_shape=tuple(jax.ShapeDtypeStruct(shape, kind) for shape in shapes),
        in_specs=[vectors] * 3,
        out_specs=(everywhere,) * 3,
        scratch_shapes=[dma((3,))],
        compiler_params=pltpu.CompilerParams(vmem_limit_bytes=1 << 20),
    )(*(pltpu.with_memory_space_constraint(x, pltpu.VMEM) for x in results))
    shape = (layers, pages, page_size, heads_here, head_size)
    return (
        key_pages.reshape(shape),
        value_pages.reshape(shape),
        attended.reshape(layers, 1, tp_size * query_heads, head_size),
    )


def solution(mesh):
    placed = (
        P(None, None, "sp", "tp", None),
        P(None, None, "sp", "tp", None),
        P(),
        P(),
        P("sp", None),
        P(None, "sp", "tp", None),
    )
    return jax.shard_map(
        functools.partial(local, mesh.shape["sp"], mesh.shape["tp"]),
        mesh=mesh,
        in_specs=placed,
        out_specs=(
            P(None, "sp", None, "tp", None),
            P(None, "sp", None, "tp", None),
            P(None, "sp", None, None),
        ),
        check_vma=False,
    )
```

profile of v0, /device:TPU:0, one launch (start us, length us, event | category | flops | bytes accessed | tf_op | source)
XLA Modules:
  0.0 34.2 jit_solution(2971727621797929273)
XLA Ops:
  0.6 32.6 %shard_map.85 = (bf16[2,32,32,128]{3,2,1,0:T(8,128)(2,1)S(1)}, bf16[2,32,32,128]{3,2,1,0:T(8,128)(2,1)S(1)}, bf16[2,64,128]{2,1,0:T(8,128)(2,1)S(1)}) custom-call(s32[8]{0:T(128)} %lengths.1, s32[8]{0:T(128)} %destination.1, s32[1,32]{1,0:T(1,128)} %table.1, bf16[2,16,128]{2,1,0:T(8,128)(2,1)} %bitcast.10, bf16[2,8,128,128]{3,2,1,0:T(8,128)(2,1)} %bitcast.8, ...), custom_call_target="tpu_custom_call" | custom-call | tf_op jit(solution)/shard_map/pallas_call | solution.py:239
  33.2 1.0 %shard_map.86 = (bf16[2,32,32,128]{3,2,1,0:T(8,128)(2,1)}, bf16[2,32,32,128]{3,2,1,0:T(8,128)(2,1)}, bf16[2,64,128]{2,1,0:T(8,128)(2,1)}) custom-call(bf16[2,32,32,128]{3,2,1,0:T(8,128)(2,1)S(1)} %get-tuple-element.9.refs_0_, bf16[2,32,32,128]{3,2,1,0:T(8,128)(2,1)S(1)} %get-tuple-element.10.refs_1_, bf16[2,64,128]{2,1,0:T(8,128)(2,1)S(1)} %get-tuple-element.11.refs_2_), custom_call_target="tpu_custom_call" | custom-call | tf_op jit(solution)/shard_map/pallas_call | solution.py:267
where the time goes:
time: 34.5 us; the launch traced here: 34.2 us
  Pallas kernels  33.6 us (97%)
  between operations  0.64 us (2%)
    pallas_call x1, Pallas kernels, local(): pl.pallas_call(functools.partial(kernel, sp_size, tp_size, page_size), ou...  32.6 us
    pallas_call x1, Pallas kernels, local(): pl.pallas_call(write_out, out_shape=tuple((jax.ShapeDtypeStruct(shape, ki...  1 us

commit v1 on v0

--- a/solution.py
+++ b/solution.py
@@ -20,12 +20,17 @@
     return total
 
 
-def turn(me, step, n):
-    if n & (n - 1) or n < 4:
+def staged(n):
+    return n >= 4 and not n & (n - 1)
+
+
+def turn(me, step, n, last):
+    if not staged(n):
         return step
-    outer = (me // (n // 4) + me // (n // 2) + 1) % 2
+    inner = (me // (n // 4) + me // (n // 2)) % 2
+    swap = 1 - inner if last else inner
     crossing = step // (n // 2)
-    return step + crossing * ((step + outer * (n // 4)) % (n // 2) + n // 2 - step)
+    return step + crossing * ((step + swap * (n // 4)) % (n // 2) + n // 2 - step)
 
 
 def kernel(
@@ -33,7 +38,7 @@
     lengths, destination, table, queries, keys_in, values_in,
     key_pages, value_pages, attended,
     fetched, outbox, inboxes, heads_out, inverse,
-    fetch_sem, send_sem, recv_sem, head_send_sem, head_recv_sem,
+    fetch_sem, send_sem, recv_sem, head_send_sem, head_recv_sem, far_sem,
 ):
     layers, prompts, rows, head_size = keys_in.shape
     per_block, page_rows = outbox.shape[3], outbox.shape[4]
@@ -81,7 +86,21 @@
         )
         return carry
 
-    lax.fori_loop(1, sp_size, greet_sp, 0)
+    half, quarter = sp_size // 2, sp_size // 4
+    split = staged(sp_size)
+    if split:
+        place_in_line, place_in_quarter = me // quarter, me % quarter
+        inner = (place_in_line + me // half) % 2
+        lax.fori_loop(1, half, greet_sp, 0)
+
+        @pl.when(inner == 1)
+        def _():
+            lax.fori_loop(half + quarter, sp_size, greet_sp, 0)
+
+        greeted = half - 1 + inner * quarter
+    else:
+        lax.fori_loop(1, sp_size, greet_sp, 0)
+        greeted = sp_size - 1
     for step in range(1, tp_size):
         pl.semaphore_signal(
             barrier, inc=1, device_id={"tp": lax.rem(row + step, tp_size)}, device_id_type=MESH
@@ -113,14 +132,44 @@
             block = fetched[layer, kind, own]
             inboxes[layer][me, kind] = block.reshape(per_block, page_rows, head_size)
 
-    pl.semaphore_wait(barrier, sp_size - 1 + tp_size - 1)
-
-    for layer in range(layers):
+    pl.semaphore_wait(barrier, greeted + tp_size - 1)
+
+    def send_steps(layer, first, stop):
         def send(step, carry):
-            block_copy(layer, turn(me, step, sp_size)).start()
+            block_copy(layer, turn(me, step, sp_size, layer == layers - 1 and layer > 0)).start()
             return carry
 
-        lax.fori_loop(1, sp_size, send, 0)
+        lax.fori_loop(first, stop, send, 0)
+
+    def pass_on(level, line):
+        pl.semaphore_signal(
+            far_sem.at[level], inc=1,
+            device_id={"sp": line * quarter + place_in_quarter}, device_id_type=MESH,
+        )
+
+    if split:
+        outward, inward = (place_in_line // 2) * 3, 3 - place_in_line
+
+        @pl.when(inner == 1)
+        def _():
+            pass_on(0, inward)
+            pass_on(0, outward)
+            send_steps(0, 1, half + quarter)
+            pl.semaphore_wait(far_sem.at[0], 1)
+            pass_on(1, outward)
+            send_steps(0, half + quarter, sp_size)
+
+        @pl.when(inner == 0)
+        def _():
+            send_steps(0, 1, half)
+            pl.semaphore_wait(far_sem.at[0], 1)
+            send_steps(0, half, half + quarter)
+            pl.semaphore_wait(far_sem.at[1], 1)
+            send_steps(0, half + quarter, sp_size)
+    else:
+        send_steps(0, 1, sp_size)
+    for layer in range(1, layers):
+        send_steps(layer, 1, sp_size)
 
     def invert(page, carry):
         def look(position, found):
@@ -145,7 +194,7 @@
 
         def attend(step, carry):
             top, total, mixed = carry
-            step = turn(me, step, sp_size)
+            step = turn(me, step, sp_size, layer == layers - 1 and layer > 0)
             source = partner(me, step, sp_size, -1)
 
             @pl.when(step > 0)
@@ -252,6 +301,7 @@
             dma((layers, sp_size)),
             dma((layers, tp_size)),
             dma((layers, tp_size)),
+            pltpu.SemaphoreType.REGULAR((2,)),
         ],
         compiler_params=pltpu.CompilerParams(
             collective_id=0, has_side_effects=True, vmem_limit_bytes=grant

time: 34.5 us -> 34.5 us (level)
  no operation moved by 1% of the time
where the time goes in v1:
time: 34.5 us; the launch traced here: 34.2 us
  Pallas kernels  33.6 us (97%)
  between operations  0.64 us (2%)
    pallas_call x1, Pallas kernels, local(): pl.pallas_call(functools.partial(kernel, sp_size, tp_size, page_size), ou...  32.6 us
    pallas_call x1, Pallas kernels, local(): pl.pallas_call(write_out, out_shape=tuple((jax.ShapeDtypeStruct(shape, ki...  1 us

profile of v1, /device:TPU:0, one launch (start us, length us, event | category | flops | bytes accessed | tf_op | source)
XLA Modules:
  0.0 34.2 jit_solution(11067373479119323930)
XLA Ops:
  0.6 32.6 %shard_map.85 = (bf16[2,32,32,128]{3,2,1,0:T(8,128)(2,1)S(1)}, bf16[2,32,32,128]{3,2,1,0:T(8,128)(2,1)S(1)}, bf16[2,64,128]{2,1,0:T(8,128)(2,1)S(1)}) custom-call(s32[8]{0:T(128)} %lengths.1, s32[8]{0:T(128)} %destination.1, s32[1,32]{1,0:T(1,128)} %table.1, bf16[2,16,128]{2,1,0:T(8,128)(2,1)} %bitcast.10, bf16[2,8,128,128]{3,2,1,0:T(8,128)(2,1)} %bitcast.8, ...), custom_call_target="tpu_custom_call" | custom-call | tf_op jit(solution)/shard_map/pallas_call | solution.py:288
  33.2 1.0 %shard_map.86 = (bf16[2,32,32,128]{3,2,1,0:T(8,128)(2,1)}, bf16[2,32,32,128]{3,2,1,0:T(8,128)(2,1)}, bf16[2,64,128]{2,1,0:T(8,128)(2,1)}) custom-call(bf16[2,32,32,128]{3,2,1,0:T(8,128)(2,1)S(1)} %get-tuple-element.9.refs_0_, bf16[2,32,32,128]{3,2,1,0:T(8,128)(2,1)S(1)} %get-tuple-element.10.refs_1_, bf16[2,64,128]{2,1,0:T(8,128)(2,1)S(1)} %get-tuple-element.11.refs_2_), custom_call_target="tpu_custom_call" | custom-call | tf_op jit(solution)/shard_map/pallas_call | solution.py:317

commit v2 on v1

--- a/solution.py
+++ b/solution.py
@@ -158,18 +158,22 @@
             pl.semaphore_wait(far_sem.at[0], 1)
             pass_on(1, outward)
             send_steps(0, half + quarter, sp_size)
+            for layer in range(1, layers):
+                send_steps(layer, 1, sp_size)
 
         @pl.when(inner == 0)
         def _():
-            send_steps(0, 1, half)
+            for layer in range(layers):
+                send_steps(layer, 1, half)
             pl.semaphore_wait(far_sem.at[0], 1)
             send_steps(0, half, half + quarter)
             pl.semaphore_wait(far_sem.at[1], 1)
             send_steps(0, half + quarter, sp_size)
+            for layer in range(1, layers):
+                send_steps(layer, half, sp_size)
     else:
-        send_steps(0, 1, sp_size)
-    for layer in range(1, layers):
-        send_steps(layer, 1, sp_size)
+        for layer in range(layers):
+            send_steps(layer, 1, sp_size)
 
     def invert(page, carry):
         def look(position, found):

time: 34.5 us -> 34.5 us (level)
  no operation moved by 1% of the time
where the time goes in v2:
time: 34.5 us; the launch traced here: 34.2 us
  Pallas kernels  33.6 us (97%)
  between operations  0.64 us (2%)
    pallas_call x1, Pallas kernels, local(): pl.pallas_call(functools.partial(kernel, sp_size, tp_size, page_size), ou...  32.6 us
    pallas_call x1, Pallas kernels, local(): pl.pallas_call(write_out, out_shape=tuple((jax.ShapeDtypeStruct(shape, ki...  1 us

profile of v2, /device:TPU:0, one launch (start us, length us, event | category | flops | bytes accessed | tf_op | source)
XLA Modules:
  0.0 34.2 jit_solution(17413852326413543165)
XLA Ops:
  0.6 32.6 %shard_map.85 = (bf16[2,32,32,128]{3,2,1,0:T(8,128)(2,1)S(1)}, bf16[2,32,32,128]{3,2,1,0:T(8,128)(2,1)S(1)}, bf16[2,64,128]{2,1,0:T(8,128)(2,1)S(1)}) custom-call(s32[8]{0:T(128)} %lengths.1, s32[8]{0:T(128)} %destination.1, s32[1,32]{1,0:T(1,128)} %table.1, bf16[2,16,128]{2,1,0:T(8,128)(2,1)} %bitcast.10, bf16[2,8,128,128]{3,2,1,0:T(8,128)(2,1)} %bitcast.8, ...), custom_call_target="tpu_custom_call" | custom-call | tf_op jit(solution)/shard_map/pallas_call | solution.py:292
  33.3 1.0 %shard_map.86 = (bf16[2,32,32,128]{3,2,1,0:T(8,128)(2,1)}, bf16[2,32,32,128]{3,2,1,0:T(8,128)(2,1)}, bf16[2,64,128]{2,1,0:T(8,128)(2,1)}) custom-call(bf16[2,32,32,128]{3,2,1,0:T(8,128)(2,1)S(1)} %get-tuple-element.9.refs_0_, bf16[2,32,32,128]{3,2,1,0:T(8,128)(2,1)S(1)} %get-tuple-element.10.refs_1_, bf16[2,64,128]{2,1,0:T(8,128)(2,1)S(1)} %get-tuple-element.11.refs_2_), custom_call_target="tpu_custom_call" | custom-call | tf_op jit(solution)/shard_map/pallas_call | solution.py:321

commit v3 on v2

--- a/solution.py
+++ b/solution.py
@@ -154,23 +154,24 @@
         def _():
             pass_on(0, inward)
             pass_on(0, outward)
-            send_steps(0, 1, half + quarter)
+            send_steps(0, half, half + quarter)
             pl.semaphore_wait(far_sem.at[0], 1)
             pass_on(1, outward)
             send_steps(0, half + quarter, sp_size)
+            send_steps(0, 1, half)
             for layer in range(1, layers):
-                send_steps(layer, 1, sp_size)
+                send_steps(layer, half, sp_size)
+                send_steps(layer, 1, half)
 
         @pl.when(inner == 0)
         def _():
-            for layer in range(layers):
-                send_steps(layer, 1, half)
+            send_steps(0, 1, half)
             pl.semaphore_wait(far_sem.at[0], 1)
             send_steps(0, half, half + quarter)
             pl.semaphore_wait(far_sem.at[1], 1)
             send_steps(0, half + quarter, sp_size)
             for layer in range(1, layers):
-                send_steps(layer, half, sp_size)
+                send_steps(layer, 1, sp_size)
     else:
         for layer in range(layers):
             send_steps(layer, 1, sp_size)
@@ -185,7 +186,8 @@
     lax.fori_loop(0, pages, invert, 0)
 
     groups = query_heads // heads_here
-    shape = (query_heads, rows)
+    joint = 2 if sp_size >= 8 and split else 1
+    shape = (query_heads, joint * rows)
     column = lax.broadcasted_iota(jnp.int32, shape, 1)
     column_head, column_token = column % heads_here, column // heads_here
     same_head = lax.broadcasted_iota(jnp.int32, shape, 0) // groups == column_head
@@ -198,15 +200,18 @@
 
         def attend(step, carry):
             top, total, mixed = carry
-            step = turn(me, step, sp_size, layer == layers - 1 and layer > 0)
-            source = partner(me, step, sp_size, -1)
+            step = turn(me, step * joint, sp_size, layer == layers - 1 and layer > 0)
+            source = partner(me, step, sp_size, -1) // joint * joint
 
             @pl.when(step > 0)
             def _():
                 block_copy(layer, step).wait_recv()
 
-            block_keys = inboxes[layer][source, 0].reshape(rows, head_size)
-            block_values = inboxes[layer][source, 1].reshape(rows, head_size)
+            for more in range(1, joint):
+                block_copy(layer, step + more).wait_recv()
+            both = pl.ds(source, joint)
+            block_keys = inboxes[layer][both, 0].reshape(joint * rows, head_size)
+            block_values = inboxes[layer][both, 1].reshape(joint * rows, head_size)
             scores = lax.dot_general(
                 asked, block_keys, (((1,), (1,)), ((), ())), preferred_element_type=jnp.float32
             ) * scale
@@ -224,7 +229,7 @@
             return new_top, total, mixed * fade + part
 
         _, total, mixed = lax.fori_loop(
-            0, sp_size, attend,
+            0, sp_size // joint, attend,
             (
                 jnp.full((query_heads, 1), -1e30, jnp.float32),
                 jnp.zeros((query_heads, 1), jnp.float32),

time: 34.5 us -> 34.5 us (level)
  no operation moved by 1% of the time
where the time goes in v3:
time: 34.5 us; the launch traced here: 34.3 us
  Pallas kernels  33.6 us (97%)
  between operations  0.64 us (2%)
    pallas_call x1, Pallas kernels, local(): pl.pallas_call(functools.partial(kernel, sp_size, tp_size, page_size), ou...  32.6 us
    pallas_call x1, Pallas kernels, local(): pl.pallas_call(write_out, out_shape=tuple((jax.ShapeDtypeStruct(shape, ki...  1 us

profile of v3, /device:TPU:0, one launch (start us, length us, event | category | flops | bytes accessed | tf_op | source)
XLA Modules:
  0.0 34.3 jit_solution(15360609636544792020)
XLA Ops:
  0.6 32.6 %shard_map.85 = (bf16[2,32,32,128]{3,2,1,0:T(8,128)(2,1)S(1)}, bf16[2,32,32,128]{3,2,1,0:T(8,128)(2,1)S(1)}, bf16[2,64,128]{2,1,0:T(8,128)(2,1)S(1)}) custom-call(s32[8]{0:T(128)} %lengths.1, s32[8]{0:T(128)} %destination.1, s32[1,32]{1,0:T(1,128)} %table.1, bf16[2,16,128]{2,1,0:T(8,128)(2,1)} %bitcast.10, bf16[2,8,128,128]{3,2,1,0:T(8,128)(2,1)} %bitcast.8, ...), custom_call_target="tpu_custom_call" | custom-call | tf_op jit(solution)/shard_map/pallas_call | solution.py:297
  33.3 1.0 %shard_map.86 = (bf16[2,32,32,128]{3,2,1,0:T(8,128)(2,1)}, bf16[2,32,32,128]{3,2,1,0:T(8,128)(2,1)}, bf16[2,64,128]{2,1,0:T(8,128)(2,1)}) custom-call(bf16[2,32,32,128]{3,2,1,0:T(8,128)(2,1)S(1)} %get-tuple-element.9.refs_0_, bf16[2,32,32,128]{3,2,1,0:T(8,128)(2,1)S(1)} %get-tuple-element.10.refs_1_, bf16[2,64,128]{2,1,0:T(8,128)(2,1)S(1)} %get-tuple-element.11.refs_2_), custom_call_target="tpu_custom_call" | custom-call | tf_op jit(solution)/shard_map/pallas_call | solution.py:326

commit v4 on v3

--- a/solution.py
+++ b/solution.py
@@ -186,7 +186,7 @@
     lax.fori_loop(0, pages, invert, 0)
 
     groups = query_heads // heads_here
-    joint = 2 if sp_size >= 8 and split else 1
+    joint = half if split else 1
     shape = (query_heads, joint * rows)
     column = lax.broadcasted_iota(jnp.int32, shape, 1)
     column_head, column_token = column % heads_here, column // heads_here
@@ -200,7 +200,7 @@
 
         def attend(step, carry):
             top, total, mixed = carry
-            step = turn(me, step * joint, sp_size, layer == layers - 1 and layer > 0)
+            step = step * joint
             source = partner(me, step, sp_size, -1) // joint * joint
 
             @pl.when(step > 0)

time: 34.5 us -> 34.5 us (level)
  no operation moved by 1% of the time
where the time goes in v4:
time: 34.5 us; the launch traced here: 34.3 us
  Pallas kernels  33.6 us (97%)
  between operations  0.64 us (2%)
    pallas_call x1, Pallas kernels, local(): pl.pallas_call(functools.partial(kernel, sp_size, tp_size, page_size), ou...  32.6 us
    pallas_call x1, Pallas kernels, local(): pl.pallas_call(write_out, out_shape=tuple((jax.ShapeDtypeStruct(shape, ki...  1 us

profile of v4, /device:TPU:0, one launch (start us, length us, event | category | flops | bytes accessed | tf_op | source)
XLA Modules:
  0.0 34.3 jit_solution(16388565797247230781)
XLA Ops:
  0.6 32.6 %shard_map.85 = (bf16[2,32,32,128]{3,2,1,0:T(8,128)(2,1)S(1)}, bf16[2,32,32,128]{3,2,1,0:T(8,128)(2,1)S(1)}, bf16[2,64,128]{2,1,0:T(8,128)(2,1)S(1)}) custom-call(s32[8]{0:T(128)} %lengths.1, s32[8]{0:T(128)} %destination.1, s32[1,32]{1,0:T(1,128)} %table.1, bf16[2,16,128]{2,1,0:T(8,128)(2,1)} %bitcast.10, bf16[2,8,128,128]{3,2,1,0:T(8,128)(2,1)} %bitcast.8, ...), custom_call_target="tpu_custom_call" | custom-call | tf_op jit(solution)/shard_map/pallas_call | solution.py:297
  33.3 1.0 %shard_map.86 = (bf16[2,32,32,128]{3,2,1,0:T(8,128)(2,1)}, bf16[2,32,32,128]{3,2,1,0:T(8,128)(2,1)}, bf16[2,64,128]{2,1,0:T(8,128)(2,1)}) custom-call(bf16[2,32,32,128]{3,2,1,0:T(8,128)(2,1)S(1)} %get-tuple-element.9.refs_0_, bf16[2,32,32,128]{3,2,1,0:T(8,128)(2,1)S(1)} %get-tuple-element.10.refs_1_, bf16[2,64,128]{2,1,0:T(8,128)(2,1)S(1)} %get-tuple-element.11.refs_2_), custom_call_target="tpu_custom_call" | custom-call | tf_op jit(solution)/shard_map/pallas_call | solution.py:326
